TPU v7x, 32 devices: a whole 2x2x4 slice. The times are simulated.
32 devices in a mesh: row: 4 (over z), col: 8 (over y, x, core).
Axes of the slice: x: 2, y: 2, z: 4, core: 2. Of those that a mesh axis runs over, the one named last changes fastest.
Arguments:
- tokens: bfloat16 [3072, 8192], P(('row', 'col')), may hold values from -6 to 6
- up_weight: bfloat16 [8192, 14336], P('row', 'col'), may hold values from -0.0625 to 0.0625
Outputs:
- projected: bfloat16 [3072, 14336], P('row', 'col')
All inputs are finite; a program needn't handle non-finite values.
Results may differ from a plain program's by a relative error of at most 0.001.
Values may be sent and summed in bfloat16 or wider, within the bound.
A program may use at most 128 MiB of HBM per device.

v0:
```python
import functools

import jax
import jax.numpy as jnp
from jax import lax
from jax.experimental import pallas as pl
from jax.experimental.pallas import tpu as pltpu
from jax.sharding import PartitionSpec as P

LINE, PLANE = 4, 8
WIDTH = 256
SPAN, OFFSET, LEAST = 250.0, 125.0, 1e-30
TS, TO, MS, MO = range(4)
MESH = pl.DeviceIdType.MESH


def gathered_weights(tokens, up_weight):
    w_column = lax.all_gather(up_weight, "row", axis=0, tiled=True)
    rows = lax.all_gather(tokens, "col", axis=0, tiled=True)
    return jnp.dot(rows, w_column, preferred_element_type=jnp.float32).astype(jnp.bfloat16)


def encode(sums):
    groups = sums.reshape(-1, 8, sums.shape[-1])
    most = jnp.maximum(jnp.max(jnp.abs(groups), axis=0), LEAST)
    code = jnp.exp2(jnp.abs(groups) * (SPAN / most)[None] - OFFSET)
    code = jnp.where(groups < 0, -code, code)
    return code.reshape(sums.shape).astype(jnp.bfloat16), most


def decode(code, most):
    groups = code.astype(jnp.float32).reshape(-1, 8, code.shape[-1])
    size = (jnp.log2(jnp.abs(groups)) + OFFSET) * (most * (1.0 / SPAN))[None]
    return jnp.where(groups < 0, -size, size).reshape(code.shape)


def kernel(
    tok, w, out, tbuf, wbuf, code_out, code_in, most_out, most_in, result,
    wl_sem, ws_sem, wr_sem, zs_sem, zr_sem, gs_sem, gr_sem, ms_sem, mr_sem, cs_sem, cr_sem, os_sem, or_sem,
):
    z, q = lax.axis_index("row"), lax.axis_index("col")
    piece, half = tok.shape[0], tok.shape[1] // 2
    depth = w.shape[0]
    chunks = wbuf.shape[0]
    rows = tbuf.shape[1]
    blocks = most_out.shape[2]
    block = rows // blocks
    mine = z // 2
    own_slot = z % 2

    def half_of(h):
        return tok.at[:, pl.ds(pl.multiple_of(h * half, half), half)]

    def place(kind, at):
        return tbuf.at[kind, pl.ds(pl.multiple_of(at * piece, piece), piece), :]

    def w_slot(j, slot):
        return wbuf.at[j, pl.ds(pl.multiple_of(slot * depth, depth), depth), :]

    def columns(ref, j):
        return ref.at[:, pl.ds(pl.multiple_of(j * WIDTH, WIDTH), WIDTH)]

    def remote(src, dst, send, recv, device):
        return pltpu.make_async_remote_copy(
            src_ref=src, dst_ref=dst, send_sem=send, recv_sem=recv, device_id=device, device_id_type=MESH
        )

    barrier = pltpu.get_barrier_semaphore()

    def greet(devices):
        for device in devices:
            pl.semaphore_signal(barrier, inc=1, device_id=device, device_id_type=MESH)
        pl.semaphore_wait(barrier, len(devices))

    @pl.when((z == 0) | (z == LINE - 1))
    def outer():
        near, beyond = 1 + mine, 2 - mine
        greet([(near, q), (beyond, q)])
        far_tokens = remote(half_of(1 - mine), place(TO, q), zs_sem.at[TO], zr_sem.at[TO], (beyond, q))
        near_tokens = remote(half_of(mine), place(MO, q), zs_sem.at[MO], zr_sem.at[MO], (near, q))
        far_tokens.start()
        near_tokens.start()

        def weight(j):
            return remote(columns(w, j), w_slot(j, own_slot), ws_sem.at[j], wr_sem.at[j], (near, q))

        @pl.loop(0, chunks)
        def _(j):
            weight(j).start()

        far_tokens.wait_send()
        near_tokens.wait_send()

        @pl.loop(0, chunks)
        def _(j):
            weight(j).wait_send()

        @pl.loop(0, chunks)
        def _(j):
            remote(result.at[1, j], columns(out, j), os_sem.at[1, j], or_sem.at[j], (near, q)).wait_recv()

    @pl.when((z != 0) & (z != LINE - 1))
    def inner():
        across = (LINE - 1 - z, q)
        end = mine * (LINE - 1)
        below, other_end = (end, q), (LINE - 1 - end, q)
        c, x, y = q % 2, (q // 2) % 2, q // 4
        over_x, over_y = q + 2 - 4 * x, q + 4 - 8 * y
        a = (1 - c) * over_x + c * over_y
        b = (1 - c) * over_y + c * over_x
        to_sib = 1 - 2 * c
        diagonal = over_x + over_y - q
        sib = q + to_sib
        greet([across, below, other_end, (z, a), (z, b), (z, sib)])

        def plane(kind, at, n, slot, device, src=None):
            here = place(kind, at)
            return remote(here if src is None else src, here, gs_sem.at[kind, n], gr_sem.at[kind, slot], (z, device))

        def own(kind, src=None):
            return [plane(kind, q, 0, 1, a, src), plane(kind, q, 1, 2, b, src), plane(kind, q, 2, 4, sib, src)]

        def from_a(kind):
            return [plane(kind, a, 3, 3, b), plane(kind, a, 4, 5, sib)]

        def from_b(kind):
            return [plane(kind, b, 5, 6, sib)]

        def from_d(kind):
            return [plane(kind, diagonal, 6, 7, sib)]

        def arrived(kind, at, slot, device):
            remote(place(kind, at), place(kind, at), gs_sem.at[kind, 0], gr_sem.at[kind, slot], (z, device)).wait_recv()

        def start(copies):
            for copy in copies:
                copy.start()

        def on_a(kind):
            arrived(kind, a, 1, a)
            start(from_a(kind))

        def on_b(kind):
            arrived(kind, b, 2, b)
            start(from_b(kind))

        def on_d(kind):
            arrived(kind, diagonal, 3, b)
            start(from_d(kind))

        def finish(kind):
            for at, slot in ((sib, 4), (b + to_sib, 5), (a + to_sib, 6), (diagonal + to_sib, 7)):
                arrived(kind, at, slot, sib)

        def z_tokens(kind, device):
            return remote(half_of(1 - mine), place(kind, q), zs_sem.at[kind], zr_sem.at[kind], device)

        def on_z(kind, device):
            z_tokens(kind, device).wait_recv()
            start(own(kind))

        own_half = half_of(mine)
        mine_here = pltpu.make_async_copy(own_half, place(MS, q), zr_sem.at[MS])

        def w_here(j):
            return pltpu.make_async_copy(columns(w, j), w_slot(j, own_slot), wl_sem.at[j])

        def w_far(j):
            return remote(columns(w, j), w_slot(j, 1 - own_slot), ws_sem.at[j], wr_sem.at[j], below)

        def sums_out(k, j):
            return [
                remote(code_out.at[k, j], code_in.at[k, j], ms_sem.at[k, j], mr_sem.at[k, j], across),
                remote(most_out.at[k, j], most_in.at[k, j], cs_sem.at[k, j], cr_sem.at[k, j], across),
            ]

        def result_up(j):
            return pltpu.make_async_copy(result.at[0, j], columns(out, j), os_sem.at[0, j])

        def result_out(j):
            return remote(result.at[1, j], columns(out, j), os_sem.at[1, j], or_sem.at[j], below)

        z_tokens(TS, across).start()
        start(own(MS, own_half))
        mine_here.start()

        @pl.loop(0, chunks)
        def _(j):
            w_here(j).start()

        on_z(TS, across)
        on_b(MS)
        on_a(TS)
        on_b(TS)
        on_z(TO, other_end)
        on_d(TS)
        finish(TS)
        on_a(TO)
        on_b(TO)
        on_a(MS)
        on_z(MO, below)
        on_d(TO)
        finish(TO)

        def product(kind, m, j):
            left = tbuf[kind, pl.ds(pl.multiple_of(m * block, block), block), :]
            return jnp.dot(left, wbuf[j], preferred_element_type=jnp.float32)

        def theirs(k, j):
            @pl.loop(0, blocks)
            def _(m):
                code, most = encode(product(TS + k, m, j))
                code_out[k, j, pl.ds(pl.multiple_of(m * block, block), block), :] = code
                most_out[k, j, m] = most

            start(sums_out(k, j))

        def finals(k, j):
            for copy in sums_out(k, j):
                copy.wait_recv()

            @pl.loop(0, blocks)
            def _(m):
                at = pl.ds(pl.multiple_of(m * block, block), block)
                total = product(MS + k, m, j) + decode(code_in[k, j, at, :], most_in[k, j, m])
                result[k, j, at, :] = total.astype(jnp.bfloat16)

        def finals_of(j):
            @pl.loop(0, 2)
            def _(n):
                k = 1 - n
                finals(k, j)

                @pl.when(k == 1)
                def _():
                    result_out(j).start()

                @pl.when(k == 0)
                def _():
                    result_up(j).start()

        @pl.loop(0, chunks + 1)
        def _(j):
            @pl.when(j < chunks)
            def _():
                w_here(j).wait()
                w_far(j).wait_recv()

                @pl.loop(0, 2)
                def _(n):
                    theirs(1 - n, j)

            @pl.when(j == 0)
            def _():
                mine_here.wait()
                on_d(MS)
                on_a(MO)
                on_b(MO)
                on_d(MO)
                finish(MS)
                finish(MO)

            @pl.when(j > 0)
            def _():
                finals_of(j - 1)

        z_tokens(TS, across).wait_send()
        for kind in range(4):
            for copy in own(kind, own_half if kind == MS else None) + from_a(kind) + from_b(kind) + from_d(kind):
                copy.wait_send()

        @pl.loop(0, chunks)
        def _(j):
            for k in range(2):
                for copy in sums_out(k, j):
                    copy.wait_send()
            result_up(j).wait()
            result_out(j).wait_send()


def line_plan(tokens, up_weight):
    piece, features = tokens.shape
    depth, columns = up_weight.shape
    rows, chunks, blocks = piece * PLANE, columns // WIDTH, 2
    dma = pltpu.SemaphoreType.DMA
    sums = (2, chunks, rows, WIDTH)
    mosts = (2, chunks, blocks, 8, WIDTH)
    return pl.pallas_call(
        kernel,
        out_shape=jax.ShapeDtypeStruct((rows, columns), jnp.bfloat16),
        in_specs=[pl.BlockSpec(memory_space=pl.ANY)] * 2,
        out_specs=pl.BlockSpec(memory_space=pl.ANY),
        scratch_shapes=[
            pltpu.VMEM((4, rows, features // 2), jnp.bfloat16),
            pltpu.VMEM((chunks, 2 * depth, WIDTH), jnp.bfloat16),
            pltpu.VMEM(sums, jnp.bfloat16),
            pltpu.VMEM(sums, jnp.bfloat16),
            pltpu.VMEM(mosts, jnp.float32),
            pltpu.VMEM(mosts, jnp.float32),
            pltpu.VMEM(sums, jnp.bfloat16),
            dma((chunks,)), dma((chunks,)), dma((chunks,)),
            dma((4,)), dma((4,)),
            dma((4, 7)), dma((4, 8)),
            dma((2, chunks)), dma((2, chunks)),
            dma((2, chunks)), dma((2, chunks)),
            dma((2, chunks)), dma((chunks,)),
        ],
        compiler_params=pltpu.CompilerParams(
            collective_id=0, has_side_effects=True, vmem_limit_bytes=67043328
        ),
        cost_estimate=pl.CostEstimate(
            flops=2 * rows * features * columns, bytes_accessed=2 * rows * features, transcendentals=0
        ),
    )(tokens, up_weight)


def solution(mesh):
    def on_device(tokens, up_weight):
        piece, features = tokens.shape
        depth, columns = up_weight.shape
        fits = mesh.shape["row"] == LINE and mesh.shape["col"] == PLANE
        fits = fits and columns % WIDTH == 0 and piece % 16 == 0 and depth % 256 == 0 and features == LINE * depth
        return (line_plan if fits else gathered_weights)(tokens, up_weight)

    return jax.shard_map(
        on_device,
        mesh=mesh,
        in_specs=(P(("row", "col"), None), P("row", "col")),
        out_specs=P("row", "col"),
        check_vma=False,
    )
```

profile of v0, /device:TPU:11, one launch (start us, length us, event | category | flops | bytes accessed | tf_op | source)
XLA Modules:
  0.0 244.7 jit_solution(17700384127829064130)
XLA Ops:
  0.0 241.2 %shard_map.28 = bf16[768,1792]{1,0:T(8,128)(2,1)} custom-call(bf16[96,8192]{1,0:T(8,128)(2,1)} %tok.1, bf16[2048,1792]{1,0:T(8,128)(2,1)} %w.1), custom_call_target="tpu_custom_call" | custom-call | flops 22548578304 | bytes 12582912 | tf_op jit(solution)/shard_map/pallas_call | solution.py:288
  241.2 3.5 %copy.4 = bf16[768,1792]{1,0:T(8,128)(2,1)} copy(bf16[768,1792]{1,0:T(8,128)(2,1)} %shard_map.28) | data formatting | bytes 5505024
where the time goes:
time: 248 us; the launch traced here: 245 us
  Pallas kernels  241 us (97%)
  local copies, waits for them, and re-layouts  3.49 us (1%)
    pallas_call x1, Pallas kernels, line_plan(): pl.pallas_call(kernel, out_shape=jax.ShapeDtypeStruct((rows, columns), jn...  241 us

commit v1 on v0

v1 whole, which is shorter than its diff:
```python
import functools

import jax
import jax.numpy as jnp
from jax import lax
from jax.experimental import pallas as pl
from jax.experimental.pallas import tpu as pltpu
from jax.sharding import PartitionSpec as P

LINE, PLANE = 4, 8
WIDTH, NARROW, FINE = 256, 128, 2
SPAN, OFFSET, LEAST = 250.0, 125.0, 1e-30
TS, TO, MS, MO = range(4)
MESH = pl.DeviceIdType.MESH


def gathered_weights(tokens, up_weight):
    w_column = lax.all_gather(up_weight, "row", axis=0, tiled=True)
    rows = lax.all_gather(tokens, "col", axis=0, tiled=True)
    return jnp.dot(rows, w_column, preferred_element_type=jnp.float32).astype(jnp.bfloat16)


def encode(sums):
    groups = sums.reshape(-1, 8, sums.shape[-1])
    most = jnp.maximum(jnp.max(jnp.abs(groups), axis=0), LEAST)
    code = jnp.exp2(jnp.abs(groups) * (SPAN / most)[None] - OFFSET)
    code = jnp.where(groups < 0, -code, code)
    return code.reshape(sums.shape).astype(jnp.bfloat16), most


def decode(code, most):
    groups = code.astype(jnp.float32).reshape(-1, 8, code.shape[-1])
    size = (jnp.log2(jnp.abs(groups)) + OFFSET) * (most * (1.0 / SPAN))[None]
    return jnp.where(groups < 0, -size, size).reshape(code.shape)


def kernel(
    tok, w, out, tbuf, mbuf, wbuf, code_out, code_in, most_out, most_in, result, acc,
    wl_sem, ws_sem, wr_sem, zs_sem, zr_sem, gs_sem, gr_sem, ms_sem, mr_sem, cs_sem, cr_sem, os_sem,
):
    z, q = lax.axis_index("row"), lax.axis_index("col")
    piece, half = tok.shape[0], tok.shape[1] // 2
    depth = w.shape[0]
    chunks = wbuf.shape[0]
    rows = tbuf.shape[1]
    blocks = most_out.shape[2]
    block = rows // blocks
    per = WIDTH // NARROW
    wide, narrow = chunks - FINE, FINE * per
    units = wide + narrow
    mine = z // 2
    own_slot = z % 2
    c, x, y = q % 2, (q // 2) % 2, q // 4
    over_x, over_y = q + 2 - 4 * x, q + 4 - 8 * y
    a = (1 - c) * over_x + c * over_y
    b = (1 - c) * over_y + c * over_x
    to_sib = 1 - 2 * c
    diagonal = over_x + over_y - q
    sib = q + to_sib
    barrier = pltpu.get_barrier_semaphore()

    def half_of(h):
        return tok.at[:, pl.ds(pl.multiple_of(h * half, half), half)]

    def block_of(k):
        return tok.at[:, pl.ds(pl.multiple_of(k * depth, depth), depth)]

    def place(kind, at):
        at = pl.ds(pl.multiple_of(at * piece, piece), piece)
        return mbuf.at[at, :] if kind == MO else tbuf.at[kind, at, :]

    def part(unit):
        if isinstance(unit, tuple):
            t = jnp.int32(unit[0])
            return wide + t, wide + lax.div(t, per), pl.ds(pl.multiple_of(lax.rem(t, per) * NARROW, NARROW), NARROW)
        return unit, unit, pl.ds(0, WIDTH)

    def columns(ref, unit):
        if isinstance(unit, tuple):
            t = jnp.int32(unit[0])
            return ref.at[:, pl.ds(pl.multiple_of(wide * WIDTH + t * NARROW, NARROW), NARROW)]
        return ref.at[:, pl.ds(pl.multiple_of(unit * WIDTH, WIDTH), WIDTH)]

    def each_unit(body):
        pl.loop(0, wide)(body)
        pl.loop(0, narrow)(lambda t: body((t,)))

    def remote(src, dst, send, recv, device):
        return pltpu.make_async_remote_copy(
            src_ref=src, dst_ref=dst, send_sem=send, recv_sem=recv, device_id=device, device_id_type=MESH
        )

    def start(copies):
        for copy in copies:
            copy.start()

    def greet(devices):
        for device in devices:
            pl.semaphore_signal(barrier, inc=1, device_id=device, device_id_type=MESH)
        pl.semaphore_wait(barrier, len(devices))

    def plane(kind, at, n, slot, device, src=None):
        here = place(kind, at)
        return remote(here if src is None else src, here, gs_sem.at[kind, n], gr_sem.at[kind, slot], (z, device))

    def own(kind, src=None):
        return [plane(kind, q, 0, 1, a, src), plane(kind, q, 1, 2, b, src), plane(kind, q, 2, 4, sib, src)]

    def from_a(kind):
        return [plane(kind, a, 3, 3, b), plane(kind, a, 4, 5, sib)]

    def from_b(kind):
        return [plane(kind, b, 5, 6, sib)]

    def from_d(kind):
        return [plane(kind, diagonal, 6, 7, sib)]

    def sent(kind, src=None):
        for copy in own(kind, src) + from_a(kind) + from_b(kind) + from_d(kind):
            copy.wait_send()

    def arrived(kind, at, slot, device):
        remote(place(kind, at), place(kind, at), gs_sem.at[kind, 0], gr_sem.at[kind, slot], (z, device)).wait_recv()

    def on_a(kind):
        arrived(kind, a, 1, a)
        start(from_a(kind))

    def on_b(kind):
        arrived(kind, b, 2, b)
        start(from_b(kind))

    def on_d(kind):
        arrived(kind, diagonal, 3, b)
        start(from_d(kind))

    def finish(kind):
        for at, slot in ((sib, 4), (b + to_sib, 5), (a + to_sib, 6), (diagonal + to_sib, 7)):
            arrived(kind, at, slot, sib)

    def w_slot(unit, slot):
        _, j, lanes = part(unit)
        return wbuf.at[j, pl.ds(pl.multiple_of(slot * depth, depth), depth), lanes]

    def w_here(j):
        at = pl.ds(pl.multiple_of(own_slot * depth, depth), depth)
        return pltpu.make_async_copy(columns(w, j), wbuf.at[j, at, :], wl_sem.at[j])

    def rows_of(m):
        return pl.ds(m * block if isinstance(m, int) else pl.multiple_of(m * block, block), block)

    def sums(k, to, unit, m, device):
        u, j, lanes = part(unit)
        at = rows_of(m)
        return [
            remote(code_out.at[k, j, at, lanes], code_in.at[to, j, at, lanes], ms_sem.at[k, u, m], mr_sem.at[to, u, m], device),
            remote(most_out.at[k, j, m, :, lanes], most_in.at[to, j, m, :, lanes], cs_sem.at[k, u, m], cr_sem.at[to, u, m], device),
        ]

    def product(kind, m, unit, slot=None):
        _, j, lanes = part(unit)
        if kind == MO:
            left, slot = mbuf[rows_of(m), :], own_slot
        elif slot is None:
            left = tbuf[kind, rows_of(m), :]
        else:
            left = tbuf[kind, rows_of(m), pl.ds(pl.multiple_of(slot * depth, depth), depth)]
        deep = slice(None) if slot is None else pl.ds(pl.multiple_of(slot * depth, depth), depth)
        return jnp.dot(left, wbuf[j, deep, lanes], preferred_element_type=jnp.float32)

    def ahead(kind, unit):
        @pl.loop(0, blocks)
        def _(m):
            acc[kind, rows_of(m), :] = product(kind, m, unit, own_slot)

    def give(kind, k, to, unit, device):
        _, j, lanes = part(unit)

        @pl.loop(0, blocks)
        def _(m):
            if kind != MO and isinstance(unit, tuple):
                total = acc[kind, rows_of(m), :] + product(kind, m, unit, 1 - own_slot)
            else:
                total = product(kind, m, unit)
            code, most = encode(total)
            code_out[k, j, rows_of(m), lanes] = code
            most_out[k, j, m, :, lanes] = most
            start(sums(k, to, unit, m, device))

    def result_up(unit):
        u, j, lanes = part(unit)
        return pltpu.make_async_copy(result.at[j, :, lanes], columns(out, unit), os_sem.at[u])

    def conclude(kind, senders, unit):
        _, j, lanes = part(unit)
        last = isinstance(unit, tuple)
        if last:
            @pl.loop(0, blocks)
            def _(m):
                acc[2, rows_of(m), :] = product(kind, m, unit)

        @pl.loop(0, blocks)
        def _(m):
            for to, device in enumerate(senders):
                for copy in sums(0, to, unit, m, device):
                    copy.wait_recv()
            total = acc[2, rows_of(m), :] if last else product(kind, m, unit)
            for to in range(len(senders)):
                total += decode(code_in[to, j, rows_of(m), lanes], most_in[to, j, m, :, lanes])
            result[j, rows_of(m), lanes] = total.astype(jnp.bfloat16)

        result_up(unit).start()

    @pl.when((z == 0) | (z == LINE - 1))
    def outer():
        near, beyond = (1 + mine, q), (2 - mine, q)
        greet([near, beyond, (z, a), (z, b), (z, sib)])
        far_tokens = remote(half_of(1 - mine), place(TO, q), zs_sem.at[TO], zr_sem.at[TO], beyond)
        near_tokens = remote(block_of(1 + mine), place(MO, q), zs_sem.at[MO], zr_sem.at[MO], near)

        def weight(unit):
            return remote(columns(w, unit), w_slot(unit, own_slot), ws_sem.at[part(unit)[0]], wr_sem.at[part(unit)[0]], near)

        near_tokens.start()
        weight(0).start()
        far_tokens.start()
        pl.loop(1, wide)(lambda j: weight(j).start())
        pl.loop(0, narrow)(lambda t: weight((t,)).start())
        start(own(MO, block_of(z)))
        mine_here = pltpu.make_async_copy(block_of(z), place(MO, q), zr_sem.at[MO])
        mine_here.start()
        pl.loop(0, chunks)(lambda j: w_here(j).start())
        on_a(MO)
        on_b(MO)
        on_d(MO)
        mine_here.wait()
        finish(MO)
        pl.loop(0, chunks)(lambda j: w_here(j).wait())
        pl.loop(0, wide)(lambda j: conclude(MO, [near, beyond], j))
        far_tokens.wait_send()
        near_tokens.wait_send()
        sent(MO, block_of(z))

        @pl.loop(0, wide)
        def _(j):
            weight(j).wait_send()
            result_up(j).wait()

        @pl.loop(0, narrow)
        def _(t):
            weight((t,)).wait_send()
            conclude(MO, [near, beyond], (t,))

        pl.loop(0, narrow)(lambda t: result_up((t,)).wait())

    @pl.when((z != 0) & (z != LINE - 1))
    def inner():
        end = mine * (LINE - 1)
        across, below, other_end = (LINE - 1 - z, q), (end, q), (LINE - 1 - end, q)
        greet([across, below, other_end, (z, a), (z, b), (z, sib)])
        own_half = half_of(mine)
        mine_here = pltpu.make_async_copy(own_half, place(MS, q), zr_sem.at[MS])

        def z_tokens(kind, device):
            src = block_of(z) if kind == MO else half_of(1 - mine)
            return remote(src, place(kind, q), zs_sem.at[kind], zr_sem.at[kind], device)

        def on_z(kind, device):
            z_tokens(kind, device).wait_recv()
            start(own(kind))

        def w_far(unit):
            u = part(unit)[0]
            return remote(columns(w, unit), w_slot(unit, 1 - own_slot), ws_sem.at[u], wr_sem.at[u], below)

        def to_across(unit):
            give(TS, 0, 0, unit, across)

        def to_other_end(unit):
            give(TO, 1, 1, unit, other_end)

        def to_below(unit):
            give(MO, 2, 0, unit, below)

        def finals(unit):
            conclude(MS, [across], unit)

        z_tokens(TS, across).start()
        mine_here.start()
        pl.loop(0, chunks)(lambda j: w_here(j).start())
        on_z(MO, below)
        on_z(TS, across)
        on_b(MO)
        on_a(TS)
        on_b(TS)
        on_d(TS)
        on_a(MO)
        finish(TS)
        pl.loop(0, chunks)(lambda j: w_here(j).wait())
        w_far(0).wait_recv()
        to_across(0)
        on_d(MO)
        on_z(TO, other_end)
        finish(MO)
        pl.loop(0, wide)(to_below)
        on_a(TO)
        on_b(TO)
        w_far(1).wait_recv()
        to_across(1)
        on_d(TO)
        start(own(MS, own_half))
        finish(TO)
        pl.loop(0, 2)(to_other_end)
        pl.loop(0, narrow)(lambda t: to_below((t,)))
        w_far(2).wait_recv()
        to_other_end(2)
        to_across(2)
        mine_here.wait()
        on_a(MS)
        on_b(MS)
        on_d(MS)
        finish(MS)
        pl.loop(0, 2)(finals)

        @pl.loop(3, wide)
        def _(j):
            w_far(j).wait_recv()
            to_other_end(j)
            to_across(j)
            finals(j - 1)

        def done(unit):
            for k, to, device in ((0, 0, across), (1, 1, other_end), (2, 0, below)):
                for m in range(blocks):
                    for copy in sums(k, to, unit, m, device):
                        copy.wait_send()

        @pl.loop(0, narrow)
        def _(t):
            ahead(TO, (t,))
            ahead(TS, (t,))
            w_far((t,)).wait_recv()
            to_other_end((t,))
            to_across((t,))

            @pl.when(t == 1)
            def _():
                finals(wide - 1)

            @pl.when(t > 1)
            def _():
                finals((t - 2,))

        z_tokens(TS, across).wait_send()
        for kind in range(4):
            sent(kind, own_half if kind == MS else None)

        @pl.loop(0, wide)
        def _(j):
            done(j)
            result_up(j).wait()

        pl.loop(narrow - 2, narrow)(lambda t: finals((t,)))

        @pl.loop(0, narrow)
        def _(t):
            done((t,))
            result_up((t,)).wait()


def line_plan(tokens, up_weight):
    piece, features = tokens.shape
    depth, columns = up_weight.shape
    rows, chunks, blocks = piece * PLANE, columns // WIDTH, 2
    units = chunks - FINE + FINE * WIDTH // NARROW
    dma, vmem, half = pltpu.SemaphoreType.DMA, pltpu.VMEM, jnp.bfloat16
    return pl.pallas_call(
        kernel,
        out_shape=jax.ShapeDtypeStruct((rows, columns), jnp.bfloat16),
        in_specs=[pl.BlockSpec(memory_space=pl.ANY)] * 2,
        out_specs=pl.BlockSpec(memory_space=pl.ANY),
        scratch_shapes=[
            vmem((3, rows, features // 2), half),
            vmem((rows, depth), half),
            vmem((chunks, 2 * depth, WIDTH), half),
            vmem((3, chunks, rows, WIDTH), half),
            vmem((2, chunks, rows, WIDTH), half),
            vmem((3, chunks, blocks, 8, WIDTH), jnp.float32),
            vmem((2, chunks, blocks, 8, WIDTH), jnp.float32),
            vmem((chunks, rows, WIDTH), half),
            vmem((3, rows, NARROW), jnp.float32),
            dma((chunks,)), dma((units,)), dma((units,)),
            dma((4,)), dma((4,)),
            dma((4, 7)), dma((4, 8)),
            dma((3, units, blocks)), dma((2, units, blocks)),
            dma((3, units, blocks)), dma((2, units, blocks)),
            dma((units,)),
        ],
        compiler_params=pltpu.CompilerParams(
            collective_id=0, has_side_effects=True, vmem_limit_bytes=67043328
        ),
        cost_estimate=pl.CostEstimate(
            flops=2 * rows * features * columns, bytes_accessed=2 * rows * features, transcendentals=0
        ),
    )(tokens, up_weight)


def solution(mesh):
    def on_device(tokens, up_weight):
        piece, features = tokens.shape
        depth, columns = up_weight.shape
        fits = columns >= (3 + FINE) * WIDTH and mesh.shape["row"] == LINE and mesh.shape["col"] == PLANE
        fits = fits and columns % WIDTH == 0 and piece % 16 == 0 and depth % 256 == 0 and features == LINE * depth
        return (line_plan if fits else gathered_weights)(tokens, up_weight)

    return jax.shard_map(
        on_device,
        mesh=mesh,
        in_specs=(P(("row", "col"), None), P("row", "col")),
        out_specs=P("row", "col"),
        check_vma=False,
    )
```

time: 248 us -> 204 us (0.82)
  Pallas kernels: 241 us -> 199 us
    pallas_call x1, Pallas kernels: 241 us -> 199 us  [line_plan(): pl.pallas_call(kernel, out_shape=jax.ShapeDtypeStruct((rows, columns), jn...]
where the time goes in v1:
time: 204 us; the launch traced here: 202 us
  Pallas kernels  199 us (98%)
  local copies, waits for them, and re-layouts  3.49 us (2%)
    pallas_call x1, Pallas kernels, line_plan(): pl.pallas_call(kernel, out_shape=jax.ShapeDtypeStruct((rows, columns), jn...  199 us

profile of v1, /device:TPU:11, one launch (start us, length us, event | category | flops | bytes accessed | tf_op | source)
XLA Modules:
  0.0 202.5 jit_solution(4110134082359685703)
XLA Ops:
  0.0 199.0 %shard_map.28 = bf16[768,1792]{1,0:T(8,128)(2,1)} custom-call(bf16[96,8192]{1,0:T(8,128)(2,1)} %tok.1, bf16[2048,1792]{1,0:T(8,128)(2,1)} %w.1), custom_call_target="tpu_custom_call" | custom-call | flops 22548578304 | bytes 12582912 | tf_op jit(solution)/shard_map/pallas_call | solution.py:377
  199.0 3.5 %copy.4 = bf16[768,1792]{1,0:T(8,128)(2,1)} copy(bf16[768,1792]{1,0:T(8,128)(2,1)} %shard_map.28) | data formatting | bytes 5505024

commit v2 on v1

v2 whole, which is shorter than its diff:
```python
import functools

import jax
import jax.numpy as jnp
from jax import lax
from jax.experimental import pallas as pl
from jax.experimental.pallas import tpu as pltpu
from jax.sharding import PartitionSpec as P

LINE, PLANE = 4, 8
WIDTH, NARROW, FINE = 256, 128, 2
SPAN, OFFSET, LEAST, GROUP = 250.0, 125.0, 1e-30, 16
TS, TO, MS, MO = range(4)
MESH = pl.DeviceIdType.MESH


def gathered_weights(tokens, up_weight):
    w_column = lax.all_gather(up_weight, "row", axis=0, tiled=True)
    rows = lax.all_gather(tokens, "col", axis=0, tiled=True)
    return jnp.dot(rows, w_column, preferred_element_type=jnp.float32).astype(jnp.bfloat16)


def encode(sums):
    groups = sums.reshape(-1, GROUP, sums.shape[-1])
    most = jnp.maximum(jnp.max(jnp.abs(groups), axis=0), LEAST).astype(jnp.bfloat16)
    code = jnp.exp2(jnp.abs(groups) * (SPAN / most.astype(jnp.float32))[None] - OFFSET)
    code = jnp.where(groups < 0, -code, code)
    return code.reshape(sums.shape).astype(jnp.bfloat16), most


def decode(code, most):
    groups = code.astype(jnp.float32).reshape(-1, GROUP, code.shape[-1])
    size = (jnp.log2(jnp.abs(groups)) + OFFSET) * (most.astype(jnp.float32) * (1.0 / SPAN))[None]
    return jnp.where(groups < 0, -size, size).reshape(code.shape)


def kernel(
    tok, w, out, tbuf, mbuf, wbuf, code_out, code_in, acc,
    wl_sem, ws_sem, wr_sem, zs_sem, zr_sem, gs_sem, gr_sem, ms_sem, mr_sem,
):
    z, q = lax.axis_index("row"), lax.axis_index("col")
    piece, half = tok.shape[0], tok.shape[1] // 2
    depth = w.shape[0]
    chunks = wbuf.shape[0]
    rows = tbuf.shape[1]
    blocks = code_out.shape[2]
    block = rows // blocks
    per = WIDTH // NARROW
    wide, narrow = chunks - FINE, FINE * per
    units = wide + narrow
    mine = z // 2
    own_slot = z % 2
    c, x, y = q % 2, (q // 2) % 2, q // 4
    over_x, over_y = q + 2 - 4 * x, q + 4 - 8 * y
    a = (1 - c) * over_x + c * over_y
    b = (1 - c) * over_y + c * over_x
    to_sib = 1 - 2 * c
    diagonal = over_x + over_y - q
    sib = q + to_sib
    barrier = pltpu.get_barrier_semaphore()

    def half_of(h):
        return tok.at[:, pl.ds(pl.multiple_of(h * half, half), half)]

    def block_of(k):
        return tok.at[:, pl.ds(pl.multiple_of(k * depth, depth), depth)]

    def place(kind, at):
        at = pl.ds(pl.multiple_of(at * piece, piece), piece)
        return mbuf.at[at, :] if kind == MO else tbuf.at[kind, at, :]

    def part(unit):
        if isinstance(unit, tuple):
            t = jnp.int32(unit[0])
            return wide + t, wide + lax.div(t, per), pl.ds(pl.multiple_of(lax.rem(t, per) * NARROW, NARROW), NARROW)
        return unit, unit, pl.ds(0, WIDTH)

    def columns(ref, unit):
        if isinstance(unit, tuple):
            t = jnp.int32(unit[0])
            return ref.at[:, pl.ds(pl.multiple_of(wide * WIDTH + t * NARROW, NARROW), NARROW)]
        return ref.at[:, pl.ds(pl.multiple_of(unit * WIDTH, WIDTH), WIDTH)]

    def each_unit(body):
        pl.loop(0, wide)(body)
        pl.loop(0, narrow)(lambda t: body((t,)))

    def remote(src, dst, send, recv, device):
        return pltpu.make_async_remote_copy(
            src_ref=src, dst_ref=dst, send_sem=send, recv_sem=recv, device_id=device, device_id_type=MESH
        )

    def start(copies):
        for copy in copies:
            copy.start()

    def greet(devices):
        for device in devices:
            pl.semaphore_signal(barrier, inc=1, device_id=device, device_id_type=MESH)
        pl.semaphore_wait(barrier, len(devices))

    def plane(kind, at, slot, device, src=None):
        here = place(kind, at)
        return remote(here if src is None else src, here, gs_sem.at[kind], gr_sem.at[kind, slot], (z, device))

    def own(kind, src=None):
        return [plane(kind, q, 0, a, src), plane(kind, q, 1, b, src), plane(kind, q, 3, sib, src)]

    def from_a(kind):
        return [plane(kind, a, 2, b), plane(kind, a, 3, sib)]

    def from_b(kind):
        return [plane(kind, b, 3, sib)]

    def from_d(kind):
        return [plane(kind, diagonal, 3, sib)]

    def pieces(kind, n):
        at = pl.ds(0, n * piece)
        return mbuf.at[at, :] if kind == MO else tbuf.at[kind, at, :]

    def sent(kind):
        remote(pieces(kind, 7), pieces(kind, 7), gs_sem.at[kind], gr_sem.at[kind, 0], (z, sib)).wait_send()

    def arrived(kind, n, slot, device):
        remote(pieces(kind, n), pieces(kind, n), gs_sem.at[kind], gr_sem.at[kind, slot], (z, device)).wait_recv()

    def on_a(kind):
        arrived(kind, 1, 0, a)
        start(from_a(kind))

    def on_b(kind):
        arrived(kind, 1, 1, b)
        start(from_b(kind))

    def on_d(kind):
        arrived(kind, 1, 2, b)
        start(from_d(kind))

    def finish(kind):
        arrived(kind, 4, 3, sib)

    def w_slot(unit, slot):
        _, j, lanes = part(unit)
        return wbuf.at[j, pl.ds(pl.multiple_of(slot * depth, depth), depth), lanes]

    def w_here(j):
        at = pl.ds(pl.multiple_of(own_slot * depth, depth), depth)
        return pltpu.make_async_copy(columns(w, j), wbuf.at[j, at, :], wl_sem.at[0])

    def rows_of(m):
        return pl.ds(m * block if isinstance(m, int) else pl.multiple_of(m * block, block), block)

    def sums(k, to, unit, m, device):
        u, j, lanes = part(unit)
        return remote(
            code_out.at[k, j, m, :, lanes], code_in.at[to, j, m, :, lanes], ms_sem.at[k], mr_sem.at[to, u, m], device
        )

    def product(kind, m, unit, slot=None):
        _, j, lanes = part(unit)
        if kind == MO:
            left, slot = mbuf[rows_of(m), :], own_slot
        elif slot is None:
            left = tbuf[kind, rows_of(m), :]
        else:
            left = tbuf[kind, rows_of(m), pl.ds(pl.multiple_of(slot * depth, depth), depth)]
        deep = slice(None) if slot is None else pl.ds(pl.multiple_of(slot * depth, depth), depth)
        return jnp.dot(left, wbuf[j, deep, lanes], preferred_element_type=jnp.float32)

    def ahead(kind, n):
        @pl.loop(0, blocks)
        def _(m):
            acc[kind, n, rows_of(m), :] = product(kind, m, wide + n, own_slot)

    def rest_of(kind, m, unit):
        _, j, lanes = part(unit)
        return acc[kind, j - wide, rows_of(m), lanes] + product(kind, m, unit, 1 - own_slot)

    def give(kind, k, to, unit, device):
        _, j, lanes = part(unit)

        @pl.loop(0, blocks)
        def _(m):
            if kind != MO and isinstance(unit, tuple):
                total = rest_of(kind, m, unit)
            else:
                total = product(kind, m, unit)
            code, most = encode(total)
            code_out[k, j, m, pl.ds(0, block), lanes] = code
            code_out[k, j, m, pl.ds(block, GROUP), lanes] = most
            sums(k, to, unit, m, device).start()

    def conclude(kind, senders, unit):
        _, j, lanes = part(unit)
        last = isinstance(unit, tuple)
        if last:
            @pl.loop(0, blocks)
            def _(m):
                acc[MS, j - wide, rows_of(m), lanes] = rest_of(kind, m, unit) if kind == MS else product(kind, m, unit)

        @pl.loop(0, blocks)
        def _(m):
            for to, device in enumerate(senders):
                sums(0, to, unit, m, device).wait_recv()
            total = acc[MS, j - wide, rows_of(m), lanes] if last else product(kind, m, unit)
            for to in range(len(senders)):
                total += decode(code_in[to, j, m, pl.ds(0, block), lanes], code_in[to, j, m, pl.ds(block, GROUP), lanes])
            at = wide * WIDTH + unit[0] * NARROW if last else unit * WIDTH
            wide_at = pl.ds(pl.multiple_of(jnp.int32(at), NARROW), NARROW if last else WIDTH)
            out[rows_of(m), wide_at] = total.astype(jnp.bfloat16)

    @pl.when((z == 0) | (z == LINE - 1))
    def outer():
        near, beyond = (1 + mine, q), (2 - mine, q)
        greet([near, beyond, (z, a), (z, b), (z, sib)])
        far_tokens = remote(half_of(1 - mine), place(TO, q), zs_sem.at[TO], zr_sem.at[TO], beyond)
        near_tokens = remote(block_of(1 + mine), place(MO, q), zs_sem.at[MO], zr_sem.at[MO], near)

        def weight(unit):
            return remote(columns(w, unit), w_slot(unit, own_slot), ws_sem.at[0], wr_sem.at[part(unit)[0]], near)

        near_tokens.start()
        weight(0).start()
        far_tokens.start()
        pl.loop(1, wide)(lambda j: weight(j).start())
        pl.loop(0, narrow)(lambda t: weight((t,)).start())
        start(own(MO, block_of(z)))
        mine_here = pltpu.make_async_copy(block_of(z), place(MO, q), zr_sem.at[MO])
        mine_here.start()
        pl.loop(0, chunks)(lambda j: w_here(j).start())
        on_a(MO)
        on_b(MO)
        on_d(MO)
        mine_here.wait()
        finish(MO)
        pltpu.make_async_copy(w, w, wl_sem.at[0]).wait()
        pl.loop(0, wide)(lambda j: conclude(MO, [near, beyond], j))
        far_tokens.wait_send()
        near_tokens.wait_send()
        sent(MO)
        remote(w, w, ws_sem.at[0], wr_sem.at[0], near).wait_send()
        pl.loop(0, narrow)(lambda t: conclude(MO, [near, beyond], (t,)))

    @pl.when((z != 0) & (z != LINE - 1))
    def inner():
        end = mine * (LINE - 1)
        across, below, other_end = (LINE - 1 - z, q), (end, q), (LINE - 1 - end, q)
        greet([across, below, other_end, (z, a), (z, b), (z, sib)])
        own_half = half_of(mine)
        mine_here = pltpu.make_async_copy(own_half, place(MS, q), zr_sem.at[MS])

        def z_tokens(kind, device):
            src = block_of(z) if kind == MO else half_of(1 - mine)
            return remote(src, place(kind, q), zs_sem.at[kind], zr_sem.at[kind], device)

        def on_z(kind, device):
            z_tokens(kind, device).wait_recv()
            start(own(kind))

        def w_far(unit):
            u = part(unit)[0]
            return remote(columns(w, unit), w_slot(unit, 1 - own_slot), ws_sem.at[0], wr_sem.at[u], below)

        def to_across(unit):
            give(TS, 0, 0, unit, across)

        def to_other_end(unit):
            give(TO, 1, 1, unit, other_end)

        def to_below(unit):
            give(MO, 2, 0, unit, below)

        def finals(unit):
            conclude(MS, [across], unit)

        z_tokens(TS, across).start()
        mine_here.start()
        pl.loop(0, chunks)(lambda j: w_here(j).start())
        on_z(MO, below)
        on_z(TS, across)
        on_b(MO)
        on_a(TS)
        on_b(TS)
        on_d(TS)
        on_a(MO)
        finish(TS)
        pltpu.make_async_copy(w, w, wl_sem.at[0]).wait()
        w_far(0).wait_recv()
        to_across(0)
        on_d(MO)
        on_z(TO, other_end)
        finish(MO)
        pl.loop(0, wide)(to_below)
        on_a(TO)
        on_b(TO)
        w_far(1).wait_recv()
        to_across(1)
        on_d(TO)
        start(own(MS, own_half))
        finish(TO)
        pl.loop(0, 2)(to_other_end)
        pl.loop(0, narrow)(lambda t: to_below((t,)))
        w_far(2).wait_recv()
        to_other_end(2)
        to_across(2)
        mine_here.wait()
        on_a(MS)
        on_b(MS)
        on_d(MS)
        finish(MS)
        pl.loop(0, 2)(finals)

        @pl.loop(3, wide)
        def _(j):
            w_far(j).wait_recv()
            to_other_end(j)
            to_across(j)
            finals(j - 1)

            @pl.when(j == 3)
            def _():
                for kind in (TO, TS, MS):
                    pl.loop(0, FINE)(lambda n: ahead(kind, n))

        @pl.loop(0, narrow)
        def _(t):
            w_far((t,)).wait_recv()
            to_other_end((t,))
            to_across((t,))

            @pl.when(t == 1)
            def _():
                finals(wide - 1)

            @pl.when(t > 1)
            def _():
                finals((t - 2,))

        z_tokens(TS, across).wait_send()
        for kind in range(4):
            sent(kind)
        pl.loop(narrow - 2, narrow)(lambda t: finals((t,)))
        for k, device in enumerate((across, other_end, below)):
            remote(code_out.at[k], code_out.at[k], ms_sem.at[k], mr_sem.at[0, 0, 0], device).wait_send()


def line_plan(tokens, up_weight):
    piece, features = tokens.shape
    depth, columns = up_weight.shape
    rows, chunks, blocks = piece * PLANE, columns // WIDTH, 2
    units = chunks - FINE + FINE * WIDTH // NARROW
    dma, vmem, half = pltpu.SemaphoreType.DMA, pltpu.VMEM, jnp.bfloat16
    return pl.pallas_call(
        kernel,
        out_shape=pltpu.VMEM((rows, columns), jnp.bfloat16),
        in_specs=[pl.BlockSpec(memory_space=pl.ANY)] * 2,
        out_specs=pl.BlockSpec(memory_space=pltpu.VMEM),
        scratch_shapes=[
            vmem((3, rows, features // 2), half),
            vmem((rows, depth), half),
            vmem((chunks, 2 * depth, WIDTH), half),
            vmem((3, chunks, blocks, rows // blocks + GROUP, WIDTH), half),
            vmem((2, chunks, blocks, rows // blocks + GROUP, WIDTH), half),
            vmem((3, FINE, rows, WIDTH), jnp.float32),
            dma((1,)), dma((1,)), dma((units,)),
            dma((4,)), dma((4,)),
            dma((4,)), dma((4, 4)),
            dma((3,)), dma((2, units, blocks)),
        ],
        compiler_params=pltpu.CompilerParams(
            collective_id=0, has_side_effects=True, vmem_limit_bytes=62914560
        ),
        cost_estimate=pl.CostEstimate(
            flops=2 * rows * features * columns, bytes_accessed=2 * rows * features, transcendentals=0
        ),
    )(tokens, up_weight)


def solution(mesh):
    def on_device(tokens, up_weight):
        piece, features = tokens.shape
        depth, columns = up_weight.shape
        fits = columns >= (4 + FINE) * WIDTH and mesh.shape["row"] == LINE and mesh.shape["col"] == PLANE
        fits = fits and columns % WIDTH == 0 and piece % 16 == 0 and depth % 256 == 0 and features == LINE * depth
        return (line_plan if fits else gathered_weights)(tokens, up_weight)

    return jax.shard_map(
        on_device,
        mesh=mesh,
        in_specs=(P(("row", "col"), None), P("row", "col")),
        out_specs=P("row", "col"),
        check_vma=False,
    )
```

time: 204 us -> 200 us (0.980)
    pallas_call x1, Pallas kernels: 199 us -> 197 us  [line_plan(): pl.pallas_call(kernel, out_shape=pltpu.VMEM((rows, columns), jnp.bfloat16...]
where the time goes in v2:
time: 200 us; the launch traced here: 198 us
  Pallas kernels  197 us (98%)
    pallas_call x1, Pallas kernels, line_plan(): pl.pallas_call(kernel, out_shape=pltpu.VMEM((rows, columns), jnp.bfloat16...  197 us

profile of v2, /device:TPU:11, one launch (start us, length us, event | category | flops | bytes accessed | tf_op | source)
XLA Modules:
  0.0 198.2 jit_solution(7993161563407723355)
XLA Ops:
  0.0 196.6 %shard_map.28 = bf16[768,1792]{1,0:T(8,128)(2,1)S(1)} custom-call(bf16[96,8192]{1,0:T(8,128)(2,1)} %tok.1, bf16[2048,1792]{1,0:T(8,128)(2,1)} %w.1), custom_call_target="tpu_custom_call" | custom-call | flops 22548578304 | bytes 12582912 | tf_op jit(solution)/shard_map/pallas_call | solution.py:354
  196.7 1.5 copy.4

commit v3 on v2

--- a/solution.py
+++ b/solution.py
@@ -36,7 +36,7 @@
 
 def kernel(
     tok, w, out, tbuf, mbuf, wbuf, code_out, code_in, acc,
-    wl_sem, ws_sem, wr_sem, zs_sem, zr_sem, gs_sem, gr_sem, ms_sem, mr_sem,
+    wl_sem, ws_sem, wr_sem, zs_sem, zr_sem, gs_sem, gr_sem, ms_sem, mr_sem, go_sem,
 ):
     z, q = lax.axis_index("row"), lax.axis_index("col")
     piece, half = tok.shape[0], tok.shape[1] // 2
@@ -144,6 +144,13 @@
         _, j, lanes = part(unit)
         return wbuf.at[j, pl.ds(pl.multiple_of(slot * depth, depth), depth), lanes]
 
+    def last_weight(n, slot, device):
+        unit, deep = (narrow - 1,), depth // 2
+        _, j, lanes = part(unit)
+        at = pl.ds(pl.multiple_of(slot * depth + n * deep, deep), deep)
+        src = columns(w.at[pl.ds(n * deep, deep), :], unit)
+        return remote(src, wbuf.at[j, at, lanes], ws_sem.at[1 + n], wr_sem.at[units - 1 + n], device)
+
     def w_here(j):
         at = pl.ds(pl.multiple_of(own_slot * depth, depth), depth)
         return pltpu.make_async_copy(columns(w, j), wbuf.at[j, at, :], wl_sem.at[0])
@@ -224,7 +231,14 @@
         weight(0).start()
         far_tokens.start()
         pl.loop(1, wide)(lambda j: weight(j).start())
-        pl.loop(0, narrow)(lambda t: weight((t,)).start())
+        pl.loop(0, narrow - 2)(lambda t: weight((t,)).start())
+
+        def last_units():
+            weight((narrow - 2,)).start()
+            for n in range(2):
+                last_weight(n, own_slot, near).start()
+
+        pl.when(c == 0)(last_units)
         start(own(MO, block_of(z)))
         mine_here = pltpu.make_async_copy(block_of(z), place(MO, q), zr_sem.at[MO])
         mine_here.start()
@@ -239,7 +253,21 @@
         far_tokens.wait_send()
         near_tokens.wait_send()
         sent(MO)
-        remote(w, w, ws_sem.at[0], wr_sem.at[0], near).wait_send()
+
+        @pl.when(c == 0)
+        def _():
+            last_weight(0, own_slot, near).wait_send()
+            pl.semaphore_signal(go_sem, inc=1, device_id=(z, sib), device_id_type=MESH)
+
+        @pl.when(c == 1)
+        def _():
+            pl.semaphore_wait(go_sem, 1)
+            last_units()
+            last_weight(0, own_slot, near).wait_send()
+
+        last_weight(1, own_slot, near).wait_send()
+        most = w.at[:, pl.ds(0, w.shape[1] - NARROW)]
+        remote(most, most, ws_sem.at[0], wr_sem.at[0], near).wait_send()
         pl.loop(0, narrow)(lambda t: conclude(MO, [near, beyond], (t,)))
 
     @pl.when((z != 0) & (z != LINE - 1))
@@ -325,7 +353,15 @@
 
         @pl.loop(0, narrow)
         def _(t):
-            w_far((t,)).wait_recv()
+            @pl.when(t < narrow - 1)
+            def _():
+                w_far((t,)).wait_recv()
+
+            @pl.when(t == narrow - 1)
+            def _():
+                for n in range(2):
+                    last_weight(n, 1 - own_slot, below).wait_recv()
+
             to_other_end((t,))
             to_across((t,))
 
@@ -348,7 +384,7 @@
 def line_plan(tokens, up_weight):
     piece, features = tokens.shape
     depth, columns = up_weight.shape
-    rows, chunks, blocks = piece * PLANE, columns // WIDTH, 2
+    rows, chunks, blocks = piece * PLANE, columns // WIDTH, 1
     units = chunks - FINE + FINE * WIDTH // NARROW
     dma, vmem, half = pltpu.SemaphoreType.DMA, pltpu.VMEM, jnp.bfloat16
     return pl.pallas_call(
@@ -363,10 +399,10 @@
             vmem((3, chunks, blocks, rows // blocks + GROUP, WIDTH), half),
             vmem((2, chunks, blocks, rows // blocks + GROUP, WIDTH), half),
             vmem((3, FINE, rows, WIDTH), jnp.float32),
-            dma((1,)), dma((1,)), dma((units,)),
+            dma((1,)), dma((3,)), dma((units + 1,)),
             dma((4,)), dma((4,)),
             dma((4,)), dma((4, 4)),
-            dma((3,)), dma((2, units, blocks)),
+            dma((3,)), dma((2, units, blocks)), pltpu.SemaphoreType.REGULAR,
         ],
         compiler_params=pltpu.CompilerParams(
             collective_id=0, has_side_effects=True, vmem_limit_bytes=62914560

time: 200 us -> 199 us (level)
  no operation moved by 1% of the time
where the time goes in v3:
time: 199 us
  Pallas kernels  197 us (99%)
    pallas_call x1, Pallas kernels, line_plan(): pl.pallas_call(kernel, out_shape=pltpu.VMEM((rows, columns), jnp.bfloat16...  197 us

profile of v3, /device:TPU:11, one launch (start us, length us, event | category | flops | bytes accessed | tf_op | source)
XLA Modules:
  0.0 198.9 jit_solution(8035591270283215044)
XLA Ops:
  0.0 197.4 %shard_map.28 = bf16[768,1792]{1,0:T(8,128)(2,1)S(1)} custom-call(bf16[96,8192]{1,0:T(8,128)(2,1)} %tok.1, bf16[2048,1792]{1,0:T(8,128)(2,1)} %w.1), custom_call_target="tpu_custom_call" | custom-call | flops 22548578304 | bytes 12582912 | tf_op jit(solution)/shard_map/pallas_call | solution.py:390
  197.4 1.5 copy.4
